TPU v7x, 32 devices: a whole 2x2x4 slice. The times are simulated.
32 devices in a mesh: seq: 8 (over z, y), chan: 4 (over x, core).
Axes of the slice: x: 2, y: 2, z: 4, core: 2. Of those that a mesh axis runs over, the one named last changes fastest.
Arguments:
- inputs: float32 [1024, 8192], P('seq', 'chan'), may hold values from -6 to 6
- conv_weight: float32 [3, 4, 8192], P(None, None, 'chan'), may hold values from -3 to 3
- conv_bias: float32 [3, 8192], P(None, 'chan'), may hold values from -1 to 1
- cotangent: float32 [1024, 8192], P('seq', 'chan'), may hold values from -6 to 6
Outputs:
- output: float32 [1024, 8192], P('seq', 'chan')
- input_grad: float32 [1024, 8192], P('seq', 'chan')
- weight_grad: float32 [3, 4, 8192], P(None, None, 'chan')
- bias_grad: float32 [3, 8192], P(None, 'chan')
All inputs are finite; a program needn't handle non-finite values.
Results may differ from a plain program's by a relative error of at most 0.0001.
Values sent between devices are 32-bit elements; how exact they have to be, the bound alone decides.
No kernel may reach another device: no remote copies, remote signals or barrier semaphores. Data moves between devices by JAX's collectives and lax.ppermute only.
A program may use at most 64 MiB of HBM per device.

v0:
```python
import jax
import jax.numpy as jnp
from jax import lax
from jax.sharding import PartitionSpec as P


def passed_along(array, axis, by):
    devices = lax.axis_size(axis)
    pairs = [(i, i + by) for i in range(devices) if 0 <= i + by < devices]
    return lax.ppermute(array, axis, pairs)


def shards(inputs, conv_weight, conv_bias, cotangent):
    shard_len = inputs.shape[0]
    layers = conv_weight.shape[0]
    taps = conv_weight.shape[1]
    act = inputs
    saved = []
    for layer in range(layers):
        before = passed_along(act[shard_len - (taps - 1) :], "seq", 1)
        padded = jnp.concatenate([before, act], axis=0)
        preact = conv_bias[layer][None, :] + sum(
            (
                conv_weight[layer, offset][None, :] * padded[offset : offset + shard_len]
                for offset in range(taps)
            )
        )
        saved.append((padded, preact))
        act = preact * jax.nn.sigmoid(preact)
    grad = cotangent
    term_list = [None] * layers
    for layer in reversed(range(layers)):
        padded, preact = saved[layer]
        gate_value = jax.nn.sigmoid(preact)
        pre_grad = grad * gate_value * (1.0 + preact * (1.0 - gate_value))
        after = passed_along(pre_grad[: taps - 1], "seq", -1)
        grad_pad = jnp.concatenate([pre_grad, after], axis=0)
        grad = sum(
            (
                conv_weight[layer, offset][None, :]
                * grad_pad[taps - 1 - offset : taps - 1 - offset + shard_len]
                for offset in range(taps)
            )
        )
        weight_terms = [
            jnp.sum(pre_grad * padded[offset : offset + shard_len], axis=0)
            for offset in range(taps)
        ]
        term_list[layer] = jnp.stack(weight_terms + [jnp.sum(pre_grad, axis=0)])
    all_terms = jnp.stack(term_list)
    summed = lax.psum(all_terms, "seq")
    return (act, grad, summed[:, :taps], summed[:, taps])


def solution(mesh):
    in_specs = (P("seq", "chan"), P(None, None, "chan"), P(None, "chan"), P("seq", "chan"))
    out_specs = (P("seq", "chan"), P("seq", "chan"), P(None, None, "chan"), P(None, "chan"))
    return jax.shard_map(shards, mesh=mesh, in_specs=in_specs, out_specs=out_specs, check_vma=False)
```

profile of v0, /device:TPU:0, one launch (start us, length us, event | category | flops | bytes accessed | tf_op | source)
XLA Modules:
  0.0 137.0 jit_solution(2371675134209580371)
XLA Ops:
  7.2 0.0 all-reduce.2.cloned.1.call-start
  7.2 0.9 slice.150
  8.1 4.9 %collective-permute-start = (f32[3,2048]{1,0:T(4,128)S(1)}, f32[3,2048]{1,0:T(4,128)S(1)}, u32[]{:S(2)}, u32[]{:S(2)}) collective-permute-start(f32[3,2048]{1,0:T(4,128)S(1)} %slice.150), channel_id=1, source_target_pairs={{0,4},{4,8},{8,12},{12,16},{16,20},{20,24},{24,28},{1,5},{5,9},{9,... | collective-permute-start | bytes 73736 | tf_op jit(solution)/shard_map/ppermute | solution.py:10
  13.0 1.1 fusion.41
  14.1 0.9 fusion.42
  15.0 0.0 collective-permute-done
  15.0 3.4 %fusion.36 = (f32[128,2048]{1,0:T(8,128)S(1)}, f32[128,2048]{1,0:T(8,128)S(1)}) fusion(f32[128,2048]{1,0:T(8,128)} %param.4, f32[2048]{0:T(1024)S(1)} %bitcast.32, f32[3,2048]{1,0:T(4,128)S(1)} %collective-permute-done, f32[2048]{0:T(1024)S(1)} %bitcast.34, f32[2048]{0:T(1024)S(1)} %bitcast.36, f32[2048]{0:T(1024)S(1)} %bitcast.38, f32[2048]{0:T(1024)S(1)} %bitcast.58), kind=kLoop, calls=%fused_computation.84 | loop fusion | flops 3932160 | bytes 3211264 | tf_op jit(solution)/shard_map/mul | solution.py:29
  18.4 3.8 %collective-permute-start.1 = (f32[3,2048]{1,0:T(4,128)S(1)}, f32[3,2048]{1,0:T(4,128)S(1)}, u32[]{:S(2)}, u32[]{:S(2)}) collective-permute-start(f32[3,2048]{1,0:T(4,128)S(1)} %slice.189), channel_id=1, source_target_pairs={{0,4},{4,8},{8,12},{12,16},{16,20},{20,24},{24,28},{1,5},{5,9},{9,... | collective-permute-start | bytes 73736 | tf_op jit(solution)/shard_map/ppermute | solution.py:10
  22.2 1.6 %collective-permute-done.1 = f32[3,2048]{1,0:T(4,128)S(1)} collective-permute-done((f32[3,2048]{1,0:T(4,128)S(1)}, f32[3,2048]{1,0:T(4,128)S(1)}, u32[]{:S(2)}, u32[]{:S(2)}) %collective-permute-start.1) | collective-permute-done | bytes 24608 | tf_op jit(solution)/shard_map/ppermute | solution.py:10
  23.8 0.0 copy-start.2
  23.8 0.7 fusion.35
  24.5 4.3 %collective-permute-start.2 = (f32[3,2048]{1,0:T(4,128)S(1)}, f32[3,2048]{1,0:T(4,128)S(1)}, u32[]{:S(2)}, u32[]{:S(2)}) collective-permute-start(f32[3,2048]{1,0:T(4,128)S(1)} %slice.194), channel_id=1, source_target_pairs={{0,4},{4,8},{8,12},{12,16},{16,20},{20,24},{24,28},{1,5},{5,9},{9,... | collective-permute-start | bytes 73736 | tf_op jit(solution)/shard_map/ppermute | solution.py:10
  28.8 1.6 %collective-permute-done.2 = f32[3,2048]{1,0:T(4,128)S(1)} collective-permute-done((f32[3,2048]{1,0:T(4,128)S(1)}, f32[3,2048]{1,0:T(4,128)S(1)}, u32[]{:S(2)}, u32[]{:S(2)}) %collective-permute-start.2) | collective-permute-done | bytes 24608 | tf_op jit(solution)/shard_map/ppermute | solution.py:10
  30.4 0.0 copy-done.2
  30.4 1.5 %fusion.38 = (f32[2048]{0:T(1024)S(1)}, f32[2048]{0:T(1024)S(1)}, f32[2048]{0:T(1024)S(1)}, f32[2048]{0:T(1024)S(1)}, f32[2048]{0:T(1024)S(1)}, /*index=5*/f32[128,2048]{1,0:T(8,128)S(1)}, f32[128,2048]{1,0:T(8,128)S(1)}) fusion(f32[128,2048]{1,0:T(8,128)S(1)} %get-tuple-element.34, f32[128,2048]{1,0:T(8,128)S(1)} %get-tuple-element.33, ...), kind=kLoop, calls=%fused_computation.89 | loop fusion | flops 8902656 | bytes 5349376 | tf_op jit(solution)/shard_map/reduce_sum | solution.py:49
  31.9 1.3 collective-permute-start.3
  33.2 5.7 %collective-permute-done.3 = f32[3,2048]{1,0:T(4,128)S(1)} collective-permute-done((f32[3,2048]{1,0:T(4,128)S(1)}, f32[3,2048]{1,0:T(4,128)S(1)}, u32[]{:S(2)}, u32[]{:S(2)}) %collective-permute-start.3) | collective-permute-done | bytes 24608 | tf_op jit(solution)/shard_map/ppermute | solution.py:10
  38.9 1.7 %fusion.37 = (f32[2048]{0:T(1024)S(1)}, f32[2048]{0:T(1024)S(1)}, f32[2048]{0:T(1024)S(1)}, f32[2048]{0:T(1024)S(1)}, f32[2048]{0:T(1024)S(1)}, /*index=5*/f32[128,2048]{1,0:T(8,128)S(1)}) fusion(f32[128,2048]{1,0:T(8,128)S(1)} %get-tuple-element.36, f32[128,2048]{1,0:T(8,128)S(1)} %get-tuple-element.35, f32[3,2048]{1,0:T(4,128)S(1)} %collective-permute-done.1, ...), kind=kLoop, calls=%fused_computation.88 | loop fusion | flops 8902656 | bytes 5365760 | tf_op jit(solution)/shard_map/reduce_sum | solution.py:49
  40.6 0.0 copy-start.1
  40.6 1.3 collective-permute-start.4
  41.9 0.0 copy-start
  41.9 1.3 fusion.34
  43.2 0.0 copy-done.1
  43.2 0.1 stack.85
  43.3 0.1 stack.78
  43.4 4.2 %collective-permute-done.4 = f32[3,2048]{1,0:T(4,128)S(1)} collective-permute-done((f32[3,2048]{1,0:T(4,128)S(1)}, f32[3,2048]{1,0:T(4,128)S(1)}, u32[]{:S(2)}, u32[]{:S(2)}) %collective-permute-start.4) | collective-permute-done | bytes 24608 | tf_op jit(solution)/shard_map/ppermute | solution.py:10
  47.6 0.0 copy-done
  47.7 3.3 %multiply_reduce_fusion.9 = (f32[2048]{0:T(1024)S(1)}, f32[2048]{0:T(1024)S(1)}, f32[2048]{0:T(1024)S(1)}, f32[2048]{0:T(1024)S(1)}, f32[2048]{0:T(1024)S(1)}, /*index=5*/f32[128,2048]{1,0:T(8,128)S(1)}) fusion(f32[128,2048]{1,0:T(8,128)S(1)} %copy-done, f32[3,2048]{1,0:T(4,128)S(1)} %collective-permute-done, f32[128,2048]{1,0:T(8,128)S(1)} %get-tuple-element.36, ...), kind=kLoop, calls=%fused_computation.73 | loop fusion | flops 7854080 | bytes 4317184 | tf_op jit(solution)/shard_map/reduce_sum | solution.py:46
  51.0 0.1 stack.71
  51.1 1.3 collective-permute-start.5
  52.4 0.8 pad_maximum_fusion.6
  53.2 0.0 all-reduce.2.cloned.1.call-update
  53.2 4.6 %collective-permute-done.5 = f32[3,2048]{1,0:T(4,128)S(1)} collective-permute-done((f32[3,2048]{1,0:T(4,128)S(1)}, f32[3,2048]{1,0:T(4,128)S(1)}, u32[]{:S(2)}, u32[]{:S(2)}) %collective-permute-start.5) | collective-permute-done | bytes 24608 | tf_op jit(solution)/shard_map/ppermute | solution.py:10
  57.8 1.4 %fusion.4 = f32[128,2048]{1,0:T(8,128)} fusion(f32[128,2048]{1,0:T(8,128)S(1)} %get-tuple-element.29, f32[3,2048]{1,0:T(4,128)S(1)} %collective-permute-done.5, f32[2048]{0:T(1024)S(1)} %bitcast.33, f32[2048]{0:T(1024)S(1)} %bitcast.35, f32[2048]{0:T(1024)S(1)} %bitcast.37, f32[2048]{0:T(1024)S(1)} %bitcast.39), kind=kLoop, calls=%fused_computation.28 | loop fusion | flops 2621440 | bytes 2154496 | tf_op jit(solution)/shard_map/add | solution.py:38
  59.3 67.9 %all-reduce.2.cloned.1.call-done = f32[3,5,2048]{2,0,1:T(4,128)} async-done(((f32[3,5,2048]{2,0,1:T(4,128)}), f32[3,5,2048]{2,0,1:T(4,128)}) %all-reduce.2.cloned.1.call-update) | async-done | bytes 122896 | tf_op jit(solution)/shard_map/psum | solution.py:51
  127.1 0.9 slice.214
  128.1 0.7 copy.8
  128.8 1.4 %slice_bitcast_fusion = f32[3,2048]{1,0:T(4,128)} fusion(f32[3,5,2048]{2,0,1:T(4,128)} %all-reduce.2.cloned.1.call-done), kind=kLoop, calls=%fused_computation.87 | loop fusion | bytes 49152 | tf_op jit(solution)/shard_map/squeeze | solution.py:52
  (8 shorter events, 0.1 us)
Async XLA Ops:
  7.2 120.0 %all-reduce.2.cloned.1.call-start = ((), (), s32[]{:S(2)}) async-start(), calls=%async_computation | async-start | bytes 327680 | tf_op jit(solution)/shard_map/psum | solution.py:51
  8.1 6.9 %collective-permute-start = (f32[3,2048]{1,0:T(4,128)S(1)}, f32[3,2048]{1,0:T(4,128)S(1)}, u32[]{:S(2)}, u32[]{:S(2)}) collective-permute-start(f32[3,2048]{1,0:T(4,128)S(1)} %slice.150), channel_id=1, source_target_pairs={{0,4},{4,8},{8,12},{12,16},{16,20},{20,24},{24,28},{1,5},{5,9},{9,... | collective-permute-start | bytes 73736 | tf_op jit(solution)/shard_map/ppermute | solution.py:10
  18.4 5.4 %collective-permute-start.1 = (f32[3,2048]{1,0:T(4,128)S(1)}, f32[3,2048]{1,0:T(4,128)S(1)}, u32[]{:S(2)}, u32[]{:S(2)}) collective-permute-start(f32[3,2048]{1,0:T(4,128)S(1)} %slice.189), channel_id=1, source_target_pairs={{0,4},{4,8},{8,12},{12,16},{16,20},{20,24},{24,28},{1,5},{5,9},{9,... | collective-permute-start | bytes 73736 | tf_op jit(solution)/shard_map/ppermute | solution.py:10
  23.8 6.6 %copy-start.2 = (f32[128,2048]{1,0:T(8,128)S(1)}, f32[128,2048]{1,0:T(8,128)}, u32[]{:S(2)}) copy-start(f32[128,2048]{1,0:T(8,128)} %param.7) | copy-start | bytes 3145732
  24.5 5.9 %collective-permute-start.2 = (f32[3,2048]{1,0:T(4,128)S(1)}, f32[3,2048]{1,0:T(4,128)S(1)}, u32[]{:S(2)}, u32[]{:S(2)}) collective-permute-start(f32[3,2048]{1,0:T(4,128)S(1)} %slice.194), channel_id=1, source_target_pairs={{0,4},{4,8},{8,12},{12,16},{16,20},{20,24},{24,28},{1,5},{5,9},{9,... | collective-permute-start | bytes 73736 | tf_op jit(solution)/shard_map/ppermute | solution.py:10
  31.9 7.0 %collective-permute-start.3 = (f32[3,2048]{1,0:T(4,128)S(1)}, f32[3,2048]{1,0:T(4,128)S(1)}, u32[]{:S(2)}, u32[]{:S(2)}) collective-permute-start(f32[3,2048]{1,0:T(4,128)S(1)} %slice.199), channel_id=1, source_target_pairs={{4,0},{8,4},{12,8},{16,12},{20,16},{24,20},{28,24},{5,1},{9,5},{13... | collective-permute-start | bytes 73736 | tf_op jit(solution)/shard_map/ppermute | solution.py:10
  40.6 2.6 %copy-start.1 = (f32[128,2048]{1,0:T(8,128)}, f32[128,2048]{1,0:T(8,128)S(1)}, u32[]{:S(2)}) copy-start(f32[128,2048]{1,0:T(8,128)S(1)} %get-tuple-element.30) | copy-start | bytes 3145732
  40.6 7.0 %collective-permute-start.4 = (f32[3,2048]{1,0:T(4,128)S(1)}, f32[3,2048]{1,0:T(4,128)S(1)}, u32[]{:S(2)}, u32[]{:S(2)}) collective-permute-start(f32[3,2048]{1,0:T(4,128)S(1)} %slice.204), channel_id=1, source_target_pairs={{4,0},{8,4},{12,8},{16,12},{20,16},{24,20},{28,24},{5,1},{9,5},{13... | collective-permute-start | bytes 73736 | tf_op jit(solution)/shard_map/ppermute | solution.py:10
  41.9 5.7 %copy-start = (f32[128,2048]{1,0:T(8,128)S(1)}, f32[128,2048]{1,0:T(8,128)}, u32[]{:S(2)}) copy-start(f32[128,2048]{1,0:T(8,128)} %param.4) | copy-start | bytes 3145732
  51.1 6.7 %collective-permute-start.5 = (f32[3,2048]{1,0:T(4,128)S(1)}, f32[3,2048]{1,0:T(4,128)S(1)}, u32[]{:S(2)}, u32[]{:S(2)}) collective-permute-start(f32[3,2048]{1,0:T(4,128)S(1)} %slice.209), channel_id=1, source_target_pairs={{4,0},{8,4},{12,8},{16,12},{20,16},{24,20},{28,24},{5,1},{9,5},{13... | collective-permute-start | bytes 73736 | tf_op jit(solution)/shard_map/ppermute | solution.py:10
Sparse Core Ops, SparseCore 0:
  53.3 73.7 all-reduce.1
where the time goes:
time: 138 us; the launch traced here: 137 us
  waiting for transfers between devices  85.6 us (62%)
  starting transfers between devices  16.9 us (12%)
  between operations  14.2 us (10%)
  other arithmetic  14.1 us (10%)
  local copies, waits for them, and re-layouts  6.21 us (4%)
    psum x1, waiting for transfers between devices, shards(): summed = lax.psum(all_terms, 'seq')  67.9 us
    ppermute x6, waiting for transfers between devices, passed_along(): return lax.ppermute(array, axis, pairs)  17.7 us
    ppermute x6, starting transfers between devices, passed_along(): return lax.ppermute(array, axis, pairs)  16.9 us
    mul x3, other arithmetic, shards(): act = preact * jax.nn.sigmoid(preact)  5.36 us
    reduce_sum x1, other arithmetic, shards(): jnp.sum(pre_grad * padded[offset:offset + shard_len], axis=0)  3.34 us
    reduce_sum x2, other arithmetic, shards(): term_list[layer] = jnp.stack(weight_terms + [jnp.sum(pre_grad, axis=0)])  3.17 us
  transfers between devices with their start and end apart: 7, of which 6 were waited for; matrix products, arithmetic and copies ran while one was open for 4% of the time, Pallas kernels for 0%

commit v1 on v0

--- a/solution.py
+++ b/solution.py
@@ -48,7 +48,7 @@
         ]
         term_list[layer] = jnp.stack(weight_terms + [jnp.sum(pre_grad, axis=0)])
     all_terms = jnp.stack(term_list)
-    summed = lax.psum(all_terms, "seq")
+    summed = jnp.sum(jax.lax.all_gather(all_terms, "seq"), axis=0)
     return (act, grad, summed[:, :taps], summed[:, taps])
 
 

time: 138 us -> 91 us (0.66)
  waiting for transfers between devices: 85.6 us -> 13.2 us
  blocking collectives: 0 us -> 40.1 us
  between operations: 14.2 us -> 0.78 us
    psum x1 -> x0, waiting for transfers between devices: 67.9 us -> none  [shards(): summed = lax.psum(all_terms, 'seq')]
    all_gather x0 -> x1, blocking collectives: none -> 40.1 us  [shards(): summed = jnp.sum(jax.lax.all_gather(all_terms, 'seq'), axis=0)]
    ppermute x6, waiting for transfers between devices: 17.7 us -> 13.2 us  [passed_along(): return lax.ppermute(array, axis, pairs)]
  transfers between devices with their start and end apart: 7 -> 6, of which waited for: 6 -> 4; matrix products, arithmetic and copies ran while one was open for 4% -> 6% of each run, Pallas kernels for 0% -> 0%
where the time goes in v1:
time: 91 us; the launch traced here: 90.5 us
  blocking collectives  40.1 us (44%)
  starting transfers between devices  16.8 us (18%)
  other arithmetic  14.3 us (16%)
  waiting for transfers between devices  13.2 us (15%)
  local copies, waits for them, and re-layouts  5.35 us (6%)
    all_gather x1, blocking collectives, shards(): summed = jnp.sum(jax.lax.all_gather(all_terms, 'seq'), axis=0)  40.1 us
    ppermute x6, starting transfers between devices, passed_along(): return lax.ppermute(array, axis, pairs)  16.8 us
    ppermute x6, waiting for transfers between devices, passed_along(): return lax.ppermute(array, axis, pairs)  13.2 us
    mul x3, other arithmetic, shards(): act = preact * jax.nn.sigmoid(preact)  5.06 us
    reduce_sum x2, other arithmetic, shards(): term_list[layer] = jnp.stack(weight_terms + [jnp.sum(pre_grad, axis=0)])  3.9 us
    reduce_sum x1, other arithmetic, shards(): jnp.sum(pre_grad * padded[offset:offset + shard_len], axis=0)  3.76 us
  transfers between devices with their start and end apart: 6, of which 4 were waited for; matrix products, arithmetic and copies ran while one was open for 6% of the time, Pallas kernels for 0%

profile of v1, /device:TPU:0, one launch (start us, length us, event | category | flops | bytes accessed | tf_op | source)
XLA Modules:
  0.0 90.5 jit_solution(1519769035003645062)
XLA Ops:
  0.6 0.9 slice.150
  1.5 4.9 %collective-permute-start = (f32[3,2048]{1,0:T(4,128)S(1)}, f32[3,2048]{1,0:T(4,128)S(1)}, u32[]{:S(2)}, u32[]{:S(2)}) collective-permute-start(f32[3,2048]{1,0:T(4,128)S(1)} %slice.150), channel_id=1, source_target_pairs={{0,4},{4,8},{8,12},{12,16},{16,20},{20,24},{24,28},{1,5},{5,9},{9,... | collective-permute-start | bytes 73736 | tf_op jit(solution)/shard_map/ppermute | solution.py:10
  6.4 1.2 %fusion.41 = (f32[1,1,2048]{2,1,0:T(1,128)S(1)}, f32[1,1,2048]{2,1,0:T(1,128)S(1)}, f32[1,1,2048]{2,1,0:T(1,128)S(1)}, f32[1,1,2048]{2,1,0:T(1,128)S(1)}, f32[1,...) fusion(f32[3,4,2048]{2,1,0:T(4,128)} %param.5), kind=kLoop, calls=%fused_computation.90 | loop fusion | bytes 196608 | tf_op jit(solution)/shard_map/slice | solution.py:24
  7.6 0.9 fusion.42
  8.5 0.0 collective-permute-done
  8.5 3.1 %fusion.36 = (f32[128,2048]{1,0:T(8,128)S(1)}, f32[128,2048]{1,0:T(8,128)S(1)}) fusion(f32[128,2048]{1,0:T(8,128)} %param.4, f32[2048]{0:T(1024)S(1)} %bitcast.41, f32[3,2048]{1,0:T(4,128)S(1)} %collective-permute-done, f32[2048]{0:T(1024)S(1)} %bitcast.43, f32[2048]{0:T(1024)S(1)} %bitcast.45, f32[2048]{0:T(1024)S(1)} %bitcast.47, f32[2048]{0:T(1024)S(1)} %bitcast.67), kind=kLoop, calls=%fused_computation.84 | loop fusion | flops 3932160 | bytes 3211264 | tf_op jit(solution)/shard_map/mul | solution.py:29
  11.6 3.7 %collective-permute-start.1 = (f32[3,2048]{1,0:T(4,128)S(1)}, f32[3,2048]{1,0:T(4,128)S(1)}, u32[]{:S(2)}, u32[]{:S(2)}) collective-permute-start(f32[3,2048]{1,0:T(4,128)S(1)} %slice.189), channel_id=1, source_target_pairs={{0,4},{4,8},{8,12},{12,16},{16,20},{20,24},{24,28},{1,5},{5,9},{9,... | collective-permute-start | bytes 73736 | tf_op jit(solution)/shard_map/ppermute | solution.py:10
  15.3 1.6 %collective-permute-done.1 = f32[3,2048]{1,0:T(4,128)S(1)} collective-permute-done((f32[3,2048]{1,0:T(4,128)S(1)}, f32[3,2048]{1,0:T(4,128)S(1)}, u32[]{:S(2)}, u32[]{:S(2)}) %collective-permute-start.1) | collective-permute-done | bytes 24608 | tf_op jit(solution)/shard_map/ppermute | solution.py:10
  16.9 0.0 copy-start.1
  16.9 0.7 fusion.35
  17.6 4.3 %collective-permute-start.2 = (f32[3,2048]{1,0:T(4,128)S(1)}, f32[3,2048]{1,0:T(4,128)S(1)}, u32[]{:S(2)}, u32[]{:S(2)}) collective-permute-start(f32[3,2048]{1,0:T(4,128)S(1)} %slice.194), channel_id=1, source_target_pairs={{0,4},{4,8},{8,12},{12,16},{16,20},{20,24},{24,28},{1,5},{5,9},{9,... | collective-permute-start | bytes 73736 | tf_op jit(solution)/shard_map/ppermute | solution.py:10
  21.9 1.6 %collective-permute-done.2 = f32[3,2048]{1,0:T(4,128)S(1)} collective-permute-done((f32[3,2048]{1,0:T(4,128)S(1)}, f32[3,2048]{1,0:T(4,128)S(1)}, u32[]{:S(2)}, u32[]{:S(2)}) %collective-permute-start.2) | collective-permute-done | bytes 24608 | tf_op jit(solution)/shard_map/ppermute | solution.py:10
  23.5 0.0 copy-done.1
  23.5 1.5 %fusion.38 = (f32[2048]{0:T(1024)S(1)}, f32[2048]{0:T(1024)S(1)}, f32[2048]{0:T(1024)S(1)}, f32[2048]{0:T(1024)S(1)}, f32[2048]{0:T(1024)S(1)}, /*index=5*/f32[128,2048]{1,0:T(8,128)S(1)}, f32[128,2048]{1,0:T(8,128)S(1)}) fusion(f32[128,2048]{1,0:T(8,128)S(1)} %get-tuple-element.38, f32[128,2048]{1,0:T(8,128)S(1)} %get-tuple-element.37, ...), kind=kLoop, calls=%fused_computation.89 | loop fusion | flops 8902656 | bytes 5349376 | tf_op jit(solution)/shard_map/reduce_sum | solution.py:49
  25.0 1.3 %collective-permute-start.3 = (f32[3,2048]{1,0:T(4,128)S(1)}, f32[3,2048]{1,0:T(4,128)S(1)}, u32[]{:S(2)}, u32[]{:S(2)}) collective-permute-start(f32[3,2048]{1,0:T(4,128)S(1)} %slice.199), channel_id=1, source_target_pairs={{4,0},{8,4},{12,8},{16,12},{20,16},{24,20},{28,24},{5,1},{9,5},{13... | collective-permute-start | bytes 73736 | tf_op jit(solution)/shard_map/ppermute | solution.py:10
  26.3 5.7 %collective-permute-done.3 = f32[3,2048]{1,0:T(4,128)S(1)} collective-permute-done((f32[3,2048]{1,0:T(4,128)S(1)}, f32[3,2048]{1,0:T(4,128)S(1)}, u32[]{:S(2)}, u32[]{:S(2)}) %collective-permute-start.3) | collective-permute-done | bytes 24608 | tf_op jit(solution)/shard_map/ppermute | solution.py:10
  32.0 2.4 %fusion.37 = (f32[2048]{0:T(1024)S(1)}, f32[2048]{0:T(1024)S(1)}, f32[2048]{0:T(1024)S(1)}, f32[2048]{0:T(1024)S(1)}, f32[2048]{0:T(1024)S(1)}, /*index=5*/f32[128,2048]{1,0:T(8,128)}) fusion(f32[128,2048]{1,0:T(8,128)S(1)} %get-tuple-element.40, f32[128,2048]{1,0:T(8,128)S(1)} %get-tuple-element.39, f32[3,2048]{1,0:T(4,128)S(1)} %collective-permute-done.1, ...), kind=kLoop, calls=%fused_computation.88 | loop fusion | flops 8902656 | bytes 5365760 | tf_op jit(solution)/shard_map/reduce_sum | solution.py:49
  34.5 0.8 slice.204
  35.3 1.3 %collective-permute-start.4 = (f32[3,2048]{1,0:T(4,128)S(1)}, f32[3,2048]{1,0:T(4,128)S(1)}, u32[]{:S(2)}, u32[]{:S(2)}) collective-permute-start(f32[3,2048]{1,0:T(4,128)S(1)} %slice.204), channel_id=1, source_target_pairs={{4,0},{8,4},{12,8},{16,12},{20,16},{24,20},{28,24},{5,1},{9,5},{13... | collective-permute-start | bytes 73736 | tf_op jit(solution)/shard_map/ppermute | solution.py:10
  36.6 0.0 copy-start
  36.6 1.3 %fusion.34 = f32[128,2048]{1,0:T(8,128)} fusion(f32[128,2048]{1,0:T(8,128)S(1)} %get-tuple-element.36), kind=kLoop, calls=%fused_computation.78 | loop fusion | flops 1048576 | bytes 2097152 | tf_op jit(solution)/shard_map/mul | solution.py:29
  37.8 0.1 stack.85
  37.9 0.1 stack.78
  38.0 4.3 %collective-permute-done.4 = f32[3,2048]{1,0:T(4,128)S(1)} collective-permute-done((f32[3,2048]{1,0:T(4,128)S(1)}, f32[3,2048]{1,0:T(4,128)S(1)}, u32[]{:S(2)}, u32[]{:S(2)}) %collective-permute-start.4) | collective-permute-done | bytes 24608 | tf_op jit(solution)/shard_map/ppermute | solution.py:10
  42.3 0.0 copy-done
  42.3 3.8 %multiply_reduce_fusion.9 = (f32[2048]{0:T(1024)S(1)}, f32[2048]{0:T(1024)S(1)}, f32[2048]{0:T(1024)S(1)}, f32[2048]{0:T(1024)S(1)}, f32[2048]{0:T(1024)S(1)}, /*index=5*/f32[128,2048]{1,0:T(8,128)S(1)}) fusion(f32[128,2048]{1,0:T(8,128)S(1)} %copy-done, f32[3,2048]{1,0:T(4,128)S(1)} %collective-permute-done, f32[128,2048]{1,0:T(8,128)S(1)} %get-tuple-element.40, ...), kind=kLoop, calls=%fused_computation.73 | loop fusion | flops 7854080 | bytes 4317184 | tf_op jit(solution)/shard_map/reduce_sum | solution.py:46
  46.1 1.3 %collective-permute-start.5 = (f32[3,2048]{1,0:T(4,128)S(1)}, f32[3,2048]{1,0:T(4,128)S(1)}, u32[]{:S(2)}, u32[]{:S(2)}) collective-permute-start(f32[3,2048]{1,0:T(4,128)S(1)} %slice.209), channel_id=1, source_target_pairs={{4,0},{8,4},{12,8},{16,12},{20,16},{24,20},{28,24},{5,1},{9,5},{13... | collective-permute-start | bytes 73736 | tf_op jit(solution)/shard_map/ppermute | solution.py:10
  47.4 0.1 stack.71
  47.5 40.1 %all-gather = f32[24,5,2048]{2,1,0:T(8,128)S(1)} all-gather(f32[3,5,2048]{2,1,0:T(8,128)S(1)} %pad_maximum_fusion.6), channel_id=2, replica_groups=mesh['seq'=8,'chan'=4] {'seq'}, dimensions={0}, use_global_device_ids=true | all-gather | bytes 1105920 | tf_op jit(solution)/shard_map/all_gather | solution.py:51
  87.6 0.1 reduce_sum.159
  87.8 0.7 slice.214
  88.4 0.6 copy.12
  89.1 0.0 collective-permute-done.5
  89.1 1.4 %fusion.4 = f32[128,2048]{1,0:T(8,128)} fusion(f32[128,2048]{1,0:T(8,128)S(1)} %get-tuple-element.33, f32[3,2048]{1,0:T(4,128)S(1)} %collective-permute-done.5, f32[2048]{0:T(1024)S(1)} %bitcast.42, f32[2048]{0:T(1024)S(1)} %bitcast.44, f32[2048]{0:T(1024)S(1)} %bitcast.46, f32[2048]{0:T(1024)S(1)} %bitcast.48), kind=kLoop, calls=%fused_computation.28 | loop fusion | flops 2621440 | bytes 2154496 | tf_op jit(solution)/shard_map/add | solution.py:38
  (6 shorter events, 0.1 us)
Async XLA Ops:
  1.5 7.0 %collective-permute-start = (f32[3,2048]{1,0:T(4,128)S(1)}, f32[3,2048]{1,0:T(4,128)S(1)}, u32[]{:S(2)}, u32[]{:S(2)}) collective-permute-start(f32[3,2048]{1,0:T(4,128)S(1)} %slice.150), channel_id=1, source_target_pairs={{0,4},{4,8},{8,12},{12,16},{16,20},{20,24},{24,28},{1,5},{5,9},{9,... | collective-permute-start | bytes 73736 | tf_op jit(solution)/shard_map/ppermute | solution.py:10
  11.6 5.3 %collective-permute-start.1 = (f32[3,2048]{1,0:T(4,128)S(1)}, f32[3,2048]{1,0:T(4,128)S(1)}, u32[]{:S(2)}, u32[]{:S(2)}) collective-permute-start(f32[3,2048]{1,0:T(4,128)S(1)} %slice.189), channel_id=1, source_target_pairs={{0,4},{4,8},{8,12},{12,16},{16,20},{20,24},{24,28},{1,5},{5,9},{9,... | collective-permute-start | bytes 73736 | tf_op jit(solution)/shard_map/ppermute | solution.py:10
  16.9 6.6 %copy-start.1 = (f32[128,2048]{1,0:T(8,128)S(1)}, f32[128,2048]{1,0:T(8,128)}, u32[]{:S(2)}) copy-start(f32[128,2048]{1,0:T(8,128)} %param.7) | copy-start | bytes 3145732
  17.6 5.9 %collective-permute-start.2 = (f32[3,2048]{1,0:T(4,128)S(1)}, f32[3,2048]{1,0:T(4,128)S(1)}, u32[]{:S(2)}, u32[]{:S(2)}) collective-permute-start(f32[3,2048]{1,0:T(4,128)S(1)} %slice.194), channel_id=1, source_target_pairs={{0,4},{4,8},{8,12},{12,16},{16,20},{20,24},{24,28},{1,5},{5,9},{9,... | collective-permute-start | bytes 73736 | tf_op jit(solution)/shard_map/ppermute | solution.py:10
  25.0 7.0 %collective-permute-start.3 = (f32[3,2048]{1,0:T(4,128)S(1)}, f32[3,2048]{1,0:T(4,128)S(1)}, u32[]{:S(2)}, u32[]{:S(2)}) collective-permute-start(f32[3,2048]{1,0:T(4,128)S(1)} %slice.199), channel_id=1, source_target_pairs={{4,0},{8,4},{12,8},{16,12},{20,16},{24,20},{28,24},{5,1},{9,5},{13... | collective-permute-start | bytes 73736 | tf_op jit(solution)/shard_map/ppermute | solution.py:10
  35.3 7.0 %collective-permute-start.4 = (f32[3,2048]{1,0:T(4,128)S(1)}, f32[3,2048]{1,0:T(4,128)S(1)}, u32[]{:S(2)}, u32[]{:S(2)}) collective-permute-start(f32[3,2048]{1,0:T(4,128)S(1)} %slice.204), channel_id=1, source_target_pairs={{4,0},{8,4},{12,8},{16,12},{20,16},{24,20},{28,24},{5,1},{9,5},{13... | collective-permute-start | bytes 73736 | tf_op jit(solution)/shard_map/ppermute | solution.py:10
  36.6 5.7 %copy-start = (f32[128,2048]{1,0:T(8,128)S(1)}, f32[128,2048]{1,0:T(8,128)}, u32[]{:S(2)}) copy-start(f32[128,2048]{1,0:T(8,128)} %param.4) | copy-start | bytes 3145732
  46.1 43.0 %collective-permute-start.5 = (f32[3,2048]{1,0:T(4,128)S(1)}, f32[3,2048]{1,0:T(4,128)S(1)}, u32[]{:S(2)}, u32[]{:S(2)}) collective-permute-start(f32[3,2048]{1,0:T(4,128)S(1)} %slice.209), channel_id=1, source_target_pairs={{4,0},{8,4},{12,8},{16,12},{20,16},{24,20},{28,24},{5,1},{9,5},{13... | collective-permute-start | bytes 73736 | tf_op jit(solution)/shard_map/ppermute | solution.py:10
